TPU v7x, 256 devices: a whole 4x4x8 slice. The times are simulated.
256 devices in a mesh: seq: 2 (over core), ctx: 32 (over x, z_hi, y), tp: 4 (over z_lo).
Axes of the slice: x: 4, y: 4, z: 8 (z_hi: 2, z_lo: 4; z = z_hi * 4 + z_lo), core: 2. Of those that a mesh axis runs over, the one named last changes fastest.
Arguments:
- queries: bfloat16 [16384, 16, 128], P(('seq', 'ctx'), 'tp'), parts along dimension 0, may hold values from -160 to 160
- key_rows: bfloat16 [16384, 4, 128], P(('seq', 'ctx'), 'tp'), parts along dimension 0, may hold values from -5 to 5
- value_slot_rows: bfloat16 [16384, 4, 128], P(('seq', 'ctx'), 'tp'), parts along dimension 0, may hold values from -6 to 6
- out_grad: bfloat16 [16384, 16, 128], P(('seq', 'ctx'), 'tp'), parts along dimension 0, may hold values from -6 to 6
- span_order: int32 [128], P('seq'), parts along dimension 0, may hold values from 0 to 63, each once
Outputs:
- query_grad: bfloat16 [16384, 16, 128], P(('seq', 'ctx'), 'tp'), parts along dimension 0
- key_gradient: bfloat16 [16384, 4, 128], P(('seq', 'ctx'), 'tp'), parts along dimension 0
- value_gradient: bfloat16 [16384, 4, 128], P(('seq', 'ctx'), 'tp'), parts along dimension 0
There are 2 independent parts, one for each index of `seq`. A program takes and returns all parts, laid end to end along the dimension named above; each array names one. Nothing has to cross between parts.
Inputs may be any that keep to these rules, and one draw needn't show every extreme that they name: Slot s of 128 rows holds span span_order[s] of the sequence; every span number stands once.
All inputs are finite; a program needn't handle non-finite values.
Results may differ from a plain program's by a relative error of at most 0.0085.
Values may be sent and summed in bfloat16 or wider, within the bound.
A program may use at most 64 MiB of HBM per device.

v0:
```python
import math

import jax
import jax.numpy as jnp
from jax import lax
from jax.sharding import PartitionSpec as P

NEGATIVE = -1e30


def in_one_piece(arrays, axis, dim, along):
    ends, at = ([], 0)
    for a in arrays[:-1]:
        at += a.shape[along]
        ends.append(at)
    both = jnp.concatenate(arrays, axis=along)
    return tuple(jnp.split(lax.all_gather(both, axis, axis=dim, tiled=True), ends, axis=along))


def sent_together(arrays, axis, dim, along):
    both = jnp.concatenate(arrays, axis=along)
    filled, at, gathered = (lax.psum_scatter(both, axis, scatter_dimension=dim, tiled=True), 0, [])
    for a in arrays:
        gathered.append(lax.slice_in_dim(filled, at, at + a.shape[along], axis=along))
        at += a.shape[along]
    return tuple(gathered)


def block_size(count):
    return math.gcd(count, 512)


def local(queries, key_rows, value_slot_rows, out_grad, span_order):
    rows_dev, query_local, head_dim = queries.shape
    kv_local = key_rows.shape[1]
    query_cluster = query_local // kv_local
    devices = lax.axis_size("ctx")
    total_rows = rows_dev * devices
    slot_count = span_order.shape[0]
    slot_rows = total_rows // slot_count
    scaling = 1.0 / math.sqrt(head_dim)
    offsets = jnp.tile(jnp.arange(slot_rows, dtype=jnp.int32), slot_count)
    places = jnp.repeat(span_order, slot_rows) * slot_rows + offsets
    my_index = lax.axis_index("ctx")
    local_places = lax.dynamic_slice_in_dim(places, my_index * rows_dev, rows_dev, 0)
    query_places = jnp.repeat(local_places, query_cluster)

    def grouped(array):
        split = array.reshape(rows_dev, kv_local, query_cluster, head_dim)
        return jnp.transpose(split, (1, 0, 2, 3)).reshape(
            kv_local, rows_dev * query_cluster, head_dim
        )

    query_group = grouped(queries)
    grad_group = grouped(out_grad)

    def block_scores(keys_part, begin):
        key_places = lax.dynamic_slice_in_dim(places, begin, keys_part.shape[0], 0)
        visible = (query_places[:, None] >= key_places[None, :])[None, :, :]
        scores = (
            jnp.einsum("hqd,khd->hqk", query_group, keys_part, preferred_element_type=jnp.float32)
            * scaling
        )
        return (visible, jnp.where(visible, scores, NEGATIVE))

    def blocked(step, carried, block_keys, block_values):
        count = block_keys.shape[0]
        block_rows = block_size(count)

        def loop_body(block_index, inner):
            offset = block_index * block_rows
            keys_part = lax.dynamic_slice_in_dim(block_keys, offset, block_rows, 0)
            values_part = lax.dynamic_slice_in_dim(block_values, offset, block_rows, 0)
            return step(inner, keys_part, values_part, offset)

        return lax.fori_loop(0, count // block_rows, loop_body, carried)

    def forward_step(state, keys_part, values_part, begin):
        running_top, running_sum, weighted = state
        visible, scores = block_scores(keys_part, begin)
        new_top = jnp.maximum(running_top, jnp.max(scores, axis=2))
        rescale = jnp.exp(running_top - new_top)
        weights = jnp.where(visible, jnp.exp(scores - new_top[..., None]), 0.0)
        running_sum = running_sum * rescale + jnp.sum(weights, axis=2)
        update = jnp.einsum(
            "hqk,khd->hqd",
            weights,
            values_part.astype(jnp.float32),
            preferred_element_type=jnp.float32,
        )
        weighted = weighted * rescale[..., None] + update
        return (new_top, running_sum, weighted)

    stat_shape = (kv_local, rows_dev * query_cluster)
    forward_init = (
        jnp.full(stat_shape, NEGATIVE, jnp.float32),
        jnp.zeros(stat_shape, jnp.float32),
        jnp.zeros(stat_shape + (head_dim,), jnp.float32),
    )
    pieces = in_one_piece((key_rows, value_slot_rows), "ctx", 0, 1)
    row_top, row_sum, weighted = blocked(forward_step, forward_init, pieces[0], pieces[1])
    log_total = row_top + jnp.log(row_sum)
    output = weighted / row_sum[..., None]
    row_delta = jnp.sum(grad_group.astype(jnp.float32) * output, axis=2)

    def backward_from(anchor):

        def backward_step(state, keys_part, values_part, begin):
            query_acc, key_complete, value_complete = state
            visible, scores = block_scores(keys_part, begin)
            probs = jnp.where(
                visible, jnp.exp(jnp.where(visible, scores - log_total[..., None], NEGATIVE)), 0.0
            )
            probs_low = probs.astype(jnp.bfloat16)
            value_block = jnp.einsum(
                "hqk,hqd->khd", probs_low, grad_group, preferred_element_type=jnp.float32
            )
            grad_probs = jnp.einsum(
                "hqd,khd->hqk", grad_group, values_part, preferred_element_type=jnp.float32
            )
            grad_scores = (probs * (grad_probs - row_delta[..., None]) * scaling).astype(
                jnp.bfloat16
            )
            query_acc = query_acc + jnp.einsum(
                "hqk,khd->hqd", grad_scores, keys_part, preferred_element_type=jnp.float32
            )
            key_block = jnp.einsum(
                "hqk,hqd->khd", grad_scores, query_group, preferred_element_type=jnp.float32
            )
            where_local = begin - anchor
            block_rows = keys_part.shape[0]
            key_before = lax.dynamic_slice_in_dim(key_complete, where_local, block_rows, 0)
            value_before = lax.dynamic_slice_in_dim(value_complete, where_local, block_rows, 0)
            key_complete = lax.dynamic_update_slice_in_dim(
                key_complete, key_before + key_block, where_local, 0
            )
            value_complete = lax.dynamic_update_slice_in_dim(
                value_complete, value_before + value_block, where_local, 0
            )
            return (query_acc, key_complete, value_complete)

        return backward_step

    query_zero = jnp.zeros(stat_shape + (head_dim,), jnp.float32)
    grad_shape = (total_rows, kv_local, head_dim)
    backward_init = (
        query_zero,
        jnp.zeros(grad_shape, jnp.float32),
        jnp.zeros(grad_shape, jnp.float32),
    )
    pieces = in_one_piece((key_rows, value_slot_rows), "ctx", 0, 1)
    query_acc, key_complete, value_complete = blocked(
        backward_from(0), backward_init, pieces[0], pieces[1]
    )
    key_sum, value_sum = sent_together((key_complete, value_complete), "ctx", 0, 1)
    query_split = query_acc.reshape(kv_local, rows_dev, query_cluster, head_dim)
    query_grad = (
        jnp.transpose(query_split, (1, 0, 2, 3))
        .reshape(rows_dev, query_local, head_dim)
        .astype(jnp.bfloat16)
    )
    return (query_grad, key_sum.astype(jnp.bfloat16), value_sum.astype(jnp.bfloat16))


def solution(mesh):
    return jax.shard_map(
        local,
        mesh=mesh,
        in_specs=(
            P(("seq", "ctx"), "tp", None),
            P(("seq", "ctx"), "tp", None),
            P(("seq", "ctx"), "tp", None),
            P(("seq", "ctx"), "tp", None),
            P("seq"),
        ),
        out_specs=(
            P(("seq", "ctx"), "tp", None),
            P(("seq", "ctx"), "tp", None),
            P(("seq", "ctx"), "tp", None),
        ),
        check_vma=False,
    )
```

profile of v0, /device:TPU:32, one launch (start us, length us, event | category | flops | bytes accessed | tf_op | source)
XLA Modules:
  0.0 606.8 jit_solution(11292710143678587831)
XLA Ops:
  9.7 116.3 %all-gather.2.cloned.1.call-done = bf16[8192,2,128]{2,0,1:T(8,128)(2,1)} async-done(((bf16[256,2,128]{2,0,1:T(8,128)(2,1)}), bf16[8192,2,128]{2,0,1:T(8,128)(2,1)}) %all-gather.2.cloned.1.call-update) | async-done | bytes 4194320 | tf_op jit(solution)/shard_map/all_gather | solution.py:17
  126.0 3.8 fusion.50
  129.8 66.8 %while.36 = (s32[]{:T(128)}, f32[1,1024]{1,0:T(1,128)S(1)}, f32[1,1024]{1,0:T(1,128)S(1)}, f32[1,1024,128]{2,1,0:T(8,128)}, s32[8192]{0:T(1024)S(1)}, /*index=5*...) while((s32[]{:T(128)}, f32[1,1024]{1,0:T(1,128)S(1)}, ...), condition=%wide.region_3.4_spmd.clone, body=%wide.region_0.3_spmd.clone.sunk | while | flops 276698112 | bytes 12160259 | solution.py:76
  198.0 2.2 broadcast.68.clone
  200.2 2.2 broadcast.68
  202.5 130.1 %while.37 = (s32[]{:T(128)}, f32[1,1024,128]{2,1,0:T(8,128)S(1)}, f32[8192,1,128]{2,0,1:T(8,128)}, f32[8192,1,128]{2,0,1:T(8,128)}, s32[8192]{0:T(1024)S(1)}, /*...) while((s32[]{:T(128)}, f32[1,1024,128]{2,1,0:T(8,128)S(1)}, ...), condition=%wide.region_6.7_spmd.clone, body=%wide.region_5.6_spmd.clone.sunk | while | flops 677249024 | bytes 13008109 | solution.py:76
  202.7 1.7 compare_select_fusion.11
  206.4 2.1 fusion.93
  208.5 2.1 fusion.92
  214.5 2.1 fusion.93
  216.7 2.1 fusion.92
  219.1 1.7 compare_select_fusion.11
  222.7 2.1 fusion.93
  224.8 2.1 fusion.92
  230.9 2.1 fusion.93
  233.0 2.1 fusion.92
  239.0 2.1 fusion.93
  241.1 2.1 fusion.92
  247.1 2.1 fusion.93
  249.2 2.1 fusion.92
  251.6 1.7 compare_select_fusion.11
  255.3 2.1 fusion.93
  257.3 2.1 fusion.92
  263.4 2.1 fusion.93
  265.5 2.1 fusion.92
  267.9 1.7 compare_select_fusion.11
  271.5 2.1 fusion.93
  273.6 2.1 fusion.92
  279.7 2.1 fusion.93
  281.8 2.1 fusion.92
  287.8 2.1 fusion.93
  289.9 2.1 fusion.92
  292.3 1.7 compare_select_fusion.11
  295.9 2.1 fusion.93
  298.0 2.1 fusion.92
  300.4 1.7 compare_select_fusion.11
  304.0 2.1 fusion.93
  306.1 2.1 fusion.92
  308.5 1.7 compare_select_fusion.11
  312.2 2.1 fusion.93
  314.3 2.1 fusion.92
  316.6 1.7 compare_select_fusion.11
  320.3 2.1 fusion.93
  322.4 2.1 fusion.92
  328.4 2.1 fusion.93
  330.5 2.1 fusion.92
  332.6 7.2 %pad_maximum_fusion = f32[8192,2,128]{2,0,1:T(8,128)} fusion(f32[8192,1,128]{2,0,1:T(8,128)} %get-tuple-element.365, f32[8192,1,128]{2,0,1:T(8,128)} %get-tuple-element.364), kind=kLoop, calls=%fused_computation.62 | loop fusion | flops 2097152 | bytes 16777216 | tf_op jit(solution)/shard_map/concatenate | solution.py:21
  340.6 257.7 %reduce-scatter.2.cloned.1.call-done = f32[256,2,128]{2,0,1:T(8,128)} async-done(((f32[8192,2,128]{2,0,1:T(8,128)}), f32[256,2,128]{2,0,1:T(8,128)}) %reduce-scatter.2.cloned.1.call-update) | async-done | bytes 262160 | tf_op jit(solution)/shard_map/reduce_scatter | solution.py:22
  (317 shorter events, 120.9 us)
Async XLA Ops:
  7.2 118.8 %all-gather.2.cloned.1.call-start = ((), (), s32[]{:S(2)}) async-start(), calls=%async_computation.1 | async-start | bytes 4325376 | tf_op jit(solution)/shard_map/all_gather | solution.py:17
  8.8 589.5 %reduce-scatter.2.cloned.1.call-start = ((), (), s32[]{:S(2)}) async-start(), calls=%async_computation.2 | async-start | bytes 8650752 | tf_op jit(solution)/shard_map/reduce_scatter | solution.py:22
  9.7 120.1 %copy-start.1 = (bf16[256,4,128]{2,1,0:T(4,128)(2,1)S(1)}, bf16[256,4,128]{2,1,0:T(4,128)(2,1)}, u32[]{:S(2)}) copy-start(bf16[256,4,128]{2,1,0:T(4,128)(2,1)} %param.9) | copy-start | bytes 786436
  129.8 66.8 %copy-start = (bf16[256,4,128]{2,1,0:T(4,128)(2,1)S(1)}, bf16[256,4,128]{2,1,0:T(4,128)(2,1)}, u32[]{:S(2)}) copy-start(bf16[256,4,128]{2,1,0:T(4,128)(2,1)} %param.12) | copy-start | bytes 786436
  130.1 2.1 copy-start.2
  133.1 0.8 copy-start.3
  134.2 2.1 copy-start.2
  137.3 0.8 copy-start.3
  138.4 2.1 copy-start.2
  141.5 0.8 copy-start.3
  142.6 2.1 copy-start.2
  145.7 0.8 copy-start.3
  146.8 2.1 copy-start.2
  149.8 0.8 copy-start.3
  151.0 2.1 copy-start.2
  154.0 0.8 copy-start.3
  155.1 2.1 copy-start.2
  158.2 0.8 copy-start.3
  159.3 2.1 copy-start.2
  162.4 0.8 copy-start.3
  163.5 2.1 copy-start.2
  166.6 0.8 copy-start.3
  167.7 2.1 copy-start.2
  170.7 0.8 copy-start.3
  171.8 2.1 copy-start.2
  174.9 0.8 copy-start.3
  176.0 2.1 copy-start.2
  179.1 0.8 copy-start.3
  180.2 2.1 copy-start.2
  183.3 0.8 copy-start.3
  184.4 2.1 copy-start.2
  187.4 0.8 copy-start.3
  188.5 2.1 copy-start.2
  191.6 0.8 copy-start.3
  192.7 2.1 copy-start.2
  195.8 0.8 copy-start.3
Sparse Core Ops, SparseCore 0:
  12.0 113.9 all-gather.1
  339.9 258.3 reduce-scatter.1
where the time goes:
time: 611 us; the launch traced here: 607 us
  waiting for transfers between devices  374 us (61%)
  matrix products  163 us (27%)
  local copies, waits for them, and re-layouts  30.8 us (5%)
  other arithmetic  23.1 us (4%)
  between operations  14.1 us (2%)
    reduce_scatter x1, waiting for transfers between devices, sent_together(): lax.psum_scatter(both, axis, scatter_dimension=dim, tiled=True)  258 us
    all_gather x1, waiting for transfers between devices, in_one_piece(): lax.all_gather(both, axis, axis=dim, tiled=True)  116 us
    dot_general x32, matrix products, block_scores(): jnp.einsum('hqd,khd->hqk', query_group, keys_part, preferred_element_type...  49.6 us
    dot_general x16, matrix products, backward_step(): jnp.einsum('hqk,hqd->khd', probs_low, grad_group, preferred_element_type=...  33.7 us
    dot_general x16, matrix products, backward_step(): jnp.einsum('hqk,hqd->khd', grad_scores, query_group, preferred_element_ty...  33.5 us
    dot_general x16, matrix products, backward_step(): jnp.einsum('hqk,khd->hqd', grad_scores, keys_part, preferred_element_type...  24.2 us
    dot_general x16, matrix products, forward_step(): jnp.einsum('hqk,khd->hqd', weights, values_part.astype(jnp.float32), pref...  14.9 us
    while x80, local copies, waits for them, and re-layouts  12.9 us
  transfers between devices with their start and end apart: 2, of which 2 were waited for; matrix products, arithmetic and copies ran while one was open for 0% of the time, Pallas kernels for 0%

commit v1 on v0

v1 whole, which is shorter than its diff:
```python
import functools
import math

import jax
import jax.numpy as jnp
from jax import lax
from jax.experimental import pallas as pl
from jax.experimental.pallas import tpu as pltpu
from jax.sharding import PartitionSpec as P

MESH = pl.DeviceIdType.MESH
SPAN = 128
HEADS = 4
DIM = 128
COLS = 2 * HEADS * SPAN
CHUNK = 4 * SPAN
HIDDEN = -1e30
F32 = jnp.float32
BF16 = jnp.bfloat16

CHUNKS = (
    ((1, 0), (3, 0)),
    ((0, 1), (0, 3)),
    ((0, 0), (2, 0)),
    ((1, 1), (1, 3)),
    ((3, 1), (3, 3)),
    ((2, 1), (2, 3)),
    ((1, 2), (3, 2)),
    ((0, 2), (2, 2)),
)
PLACE = {
    (da, db): (chunk, pos)
    for chunk, pair in enumerate(CHUNKS)
    for pos, (da, db) in enumerate(pair)
}


def slot_of(base, colour, da, db):
    chunk, pos = PLACE[(da % 4, db % 4)]
    return base + chunk * 4 + colour * 2 + pos


def kernel(
    span_ref, q_ref, g_ref, k_ref, v_ref,
    dq_ref, dk_ref, dv_ref,
    kv, part, stage, half_in, full_in, ring_in, z_in,
    qt, gt, qrows, grows, lhs, pbuf, dsbuf, dqt, top, total, delta, spans,
    load_sem, gather_send, gather_recv, gather_z, reduce_send, reduce_recv, reduce_z,
):
    me = lax.axis_index("ctx")
    x, z, y = me // 8, (me // 4) % 2, me % 4

    def at(xx, zz, yy):
        return (xx % 4) * 8 + (zz % 2) * 4 + yy % 4

    x_up, x_down = at(x + 1, z, y), at(x + 3, z, y)
    y_up, y_down = at(x, z, y + 1), at(x, z, y + 3)
    z_other = at(x, z + 1, y)
    ring_a = ((x_up, x_down), (y_up, y_down))
    ring_b = ((y_up, y_down), (x_up, x_down))

    loads = []
    for colour in range(2):
        own = slot_of(0, colour, 0, 0)
        rows = pl.ds(colour * SPAN, SPAN)
        loads.append(pltpu.make_async_copy(k_ref.at[rows], kv.at[own, 0], load_sem.at[2 * colour]))
        loads.append(
            pltpu.make_async_copy(v_ref.at[rows], kv.at[own, 1], load_sem.at[2 * colour + 1])
        )
    for copy in loads:
        copy.start()

    barrier = pltpu.get_barrier_semaphore()
    for other in (x_up, x_down, y_up, y_down, z_other):
        pl.semaphore_signal(barrier, inc=1, device_id={"ctx": other}, device_id_type=MESH)
    pl.semaphore_wait(barrier, 5)
    for copy in loads:
        copy.wait()

    def send(src, dst, send_sem, recv_sem, device):
        pltpu.make_async_remote_copy(
            src_ref=src, dst_ref=dst, send_sem=send_sem, recv_sem=recv_sem,
            device_id={"ctx": device}, device_id_type=MESH,
        ).start()

    def await_units(sem, units):
        block = kv.at[pl.ds(0, units)]
        pltpu.make_async_copy(block, block, sem).wait()

    def gather(dz, group, src, dst, device):
        send(src, dst, gather_send, gather_recv.at[dz, group], device)

    def gather_own(base, dz):
        for c in range(2):
            own = kv.at[slot_of(base, c, 0, 0)]
            gather(dz, 0, own, kv.at[slot_of(base, c, 3, 0)], ring_a[c][0])
            gather(dz, 0, own, kv.at[slot_of(base, c, 1, 0)], ring_a[c][1])
        gather_second(base, dz, 1, 0)

    def gather_second(base, dz, group, da):
        for c in range(2):
            unit = kv.at[slot_of(base, c, da, 0)]
            gather(dz, group, unit, kv.at[slot_of(base, c, da, 3)], ring_b[c][0])
            gather(dz, group, unit, kv.at[slot_of(base, c, da, 1)], ring_b[c][1])

    def gather_first_opposite(base, dz):
        for c in range(2):
            there = slot_of(base, c, 2, 0)
            gather(dz, 2, kv.at[slot_of(base, c, 3, 0), 0], kv.at[there, 0], ring_a[c][0])
            gather(dz, 2, kv.at[slot_of(base, c, 1, 0), 1], kv.at[there, 1], ring_a[c][1])

    def gather_second_opposite(base, dz, group, da):
        for c in range(2):
            there = slot_of(base, c, da, 2)
            gather(dz, group, kv.at[slot_of(base, c, da, 3), 0], kv.at[there, 0], ring_b[c][0])
            gather(dz, group, kv.at[slot_of(base, c, da, 1), 1], kv.at[there, 1], ring_b[c][1])

    for c in range(2):
        send(
            kv.at[slot_of(0, c, 0, 0)], kv.at[slot_of(32, c, 0, 0)],
            gather_send, gather_z, z_other,
        )
    gather_own(0, 0)

    for dz in range(2):
        for da in range(4):
            for db in range(4):
                for c in range(2):
                    dx, dy = (da, db) if c == 0 else (db, da)
                    owner = at(x + dx, z + dz, y + dy)
                    spans[slot_of(32 * dz, c, da, db)] = span_ref[owner * 2 + c]
    mine = [span_ref[me * 2 + s] for s in range(2)]

    lane = lax.broadcasted_iota(jnp.int32, (SPAN, SPAN), 1)
    sublane = lax.broadcasted_iota(jnp.int32, (SPAN, SPAN), 0)
    identity = jnp.where(lane == sublane, 1.0, 0.0).astype(BF16)
    for s in range(2):
        for h in range(HEADS):
            rows = pl.ds(s * SPAN, SPAN)
            heads = pl.ds(h * DIM, DIM)
            here = pl.ds((s * HEADS + h) * SPAN, SPAN)
            q_block, g_block = q_ref[rows, heads], g_ref[rows, heads]
            qrows[here, :] = q_block
            grows[here, :] = g_block
            qt[0:DIM, here] = q_block.astype(F32).T.astype(BF16)
            gt[:, here] = g_block.astype(F32).T.astype(BF16)
            qt[DIM : 2 * DIM, here] = identity
    top[...] = jnp.full_like(top, HIDDEN)
    total[...] = jnp.zeros_like(total)
    delta[...] = jnp.zeros_like(delta)
    dqt[...] = jnp.zeros_like(dqt)

    exponent = math.log2(math.e) / math.sqrt(DIM)

    def load_chunk(chunk):
        keys = kv[pl.ds(chunk * 4, 4), 0].reshape(CHUNK, DIM)
        values = kv[pl.ds(chunk * 4, 4), 1].reshape(CHUNK, DIM)
        ahead = sublane - lane
        for s in range(2):
            lhs[s, :, 0:DIM] = keys
            for u in range(4):
                limit = (mine[s] - spans[chunk * 4 + u]) * SPAN
                lhs[s, u * SPAN : (u + 1) * SPAN, DIM : 2 * DIM] = jnp.where(
                    ahead > limit, HIDDEN, 0.0
                ).astype(BF16)
        return keys, values

    WIDE = 256
    TILES = COLS // WIDE

    def scores(tile):
        cols = pl.ds(tile * WIDE, WIDE)
        s = tile * WIDE // (HEADS * SPAN)
        return cols, jnp.dot(lhs[s], qt[:, cols], preferred_element_type=F32)

    def fold(values, op):
        return op(values.reshape(CHUNK // 8, 8, WIDE), axis=0)

    def forward(chunk, _):
        dz, step = chunk // 8, chunk % 8
        base = dz * 32

        @pl.when(step == 0)
        def _():
            await_units(gather_recv.at[dz, 0], 4)
            gather_first_opposite(base, dz)
            gather_second(base, dz, 3, 1)
            gather_second(base, dz, 4, 3)

        @pl.when(step == 1)
        def _():
            await_units(gather_recv.at[dz, 1], 4)
            gather_second_opposite(base, dz, 6, 0)

        @pl.when(step == 2)
        def _():
            await_units(gather_recv.at[dz, 2], 2)
            gather_second(base, dz, 5, 2)

        @pl.when(step == 3)
        def _():
            await_units(gather_recv.at[dz, 3], 4)
            gather_second_opposite(base, dz, 7, 1)

        @pl.when(step == 4)
        def _():
            await_units(gather_recv.at[dz, 4], 4)
            gather_second_opposite(base, dz, 8, 3)

        @pl.when(step == 5)
        def _():
            await_units(gather_recv.at[dz, 5], 4)
            gather_second_opposite(base, dz, 9, 2)

        @pl.when(chunk == 6)
        def _():
            await_units(gather_z, 2)
            gather_own(32, 1)

        @pl.when(step == 6)
        def _():
            await_units(gather_recv.at[dz, 7], 2)
            await_units(gather_recv.at[dz, 8], 2)

        @pl.when(step == 7)
        def _():
            await_units(gather_recv.at[dz, 6], 2)
            await_units(gather_recv.at[dz, 9], 2)

        keys, values = load_chunk(chunk)
        for tile in range(TILES):
            cols, score = scores(tile)
            grad_probs = jnp.dot(values, gt[:, cols], preferred_element_type=F32)
            before = top[:, cols]
            now = jnp.maximum(before, jnp.max(fold(score, jnp.max), axis=0, keepdims=True))
            rescale = jnp.exp2((before - now) * exponent)
            weights = jnp.exp2((score - now) * exponent)
            top[:, cols] = now
            total[:, cols] = total[:, cols] * rescale + fold(weights, jnp.sum)
            delta[:, cols] = delta[:, cols] * rescale + fold(weights * grad_probs, jnp.sum)
        return 0

    lax.fori_loop(0, 16, forward, 0)

    weight = jnp.sum(total[...], axis=0, keepdims=True)
    row_delta = jnp.sum(delta[...], axis=0, keepdims=True) / weight
    top[...] = top[...] + jnp.log(weight) * math.sqrt(DIM)
    delta[0:1, :] = row_delta

    def reduce(dz, group, src, dst, device):
        send(src, dst, reduce_send, reduce_recv.at[dz, group], device)

    def send_halves(base, dz, da):
        for c in range(2):
            slot = slot_of(base, c, da, 2)
            stage[slot] = part[slot].astype(BF16)
            up, down = ring_b[c]
            reduce(dz, da, stage.at[slot, 0], half_in.at[slot_of(base, c, da, 1)], up)
            reduce(dz, da, stage.at[slot, 1], half_in.at[slot_of(base, c, da, 3)], down)

    def add_half(slot, which, sums):
        arrived = half_in[slot].astype(F32)
        return [sums[0] + arrived, sums[1]] if which == 0 else [sums[0], sums[1] + arrived]

    def put(slot, sums):
        stage[slot, 0] = sums[0].astype(BF16)
        stage[slot, 1] = sums[1].astype(BF16)

    def send_second(base, dz, da):
        await_units(reduce_recv.at[dz, da], 2)
        for c in range(2):
            for way, db in enumerate((1, 3)):
                slot = slot_of(base, c, da, db)
                put(slot, add_half(slot, way, [part[slot, 0], part[slot, 1]]))
                reduce(dz, 4 + da, stage.at[slot], full_in.at[dz, da, c, way], ring_b[c][way])

    def second_sum(base, dz, c, da):
        slot = slot_of(base, c, da, 0)
        return slot, [
            part[slot, i]
            + full_in[dz, da, c, 0, i].astype(F32)
            + full_in[dz, da, c, 1, i].astype(F32)
            for i in range(2)
        ]

    def send_first_halves(base, dz):
        await_units(reduce_recv.at[dz, 6], 4)
        for c in range(2):
            slot, sums = second_sum(base, dz, c, 2)
            put(slot, sums)
            up, down = ring_a[c]
            reduce(dz, 8, stage.at[slot, 0], half_in.at[slot_of(base, c, 1, 0)], up)
            reduce(dz, 8, stage.at[slot, 1], half_in.at[slot_of(base, c, 3, 0)], down)

    def send_first(base, dz):
        await_units(reduce_recv.at[dz, 5], 4)
        await_units(reduce_recv.at[dz, 7], 4)
        await_units(reduce_recv.at[dz, 8], 2)
        for c in range(2):
            for way, da in enumerate((1, 3)):
                slot, sums = second_sum(base, dz, c, da)
                put(slot, add_half(slot, way, sums))
                reduce(dz, 9, stage.at[slot], ring_in.at[dz, c, way], ring_a[c][way])

    def own_sum(base, dz, c):
        slot, sums = second_sum(base, dz, c, 0)
        return slot, [
            sums[i] + ring_in[dz, c, 0, i].astype(F32) + ring_in[dz, c, 1, i].astype(F32)
            for i in range(2)
        ]

    scaling = 1.0 / math.sqrt(DIM)

    def backward(turn, _):
        chunk = 15 - turn
        dz, step = 1 - turn // 8, turn % 8
        base = dz * 32
        keys, values = load_chunk(chunk)
        for tile in range(TILES):
            cols, score = scores(tile)
            grad_probs = jnp.dot(values, gt[:, cols], preferred_element_type=F32)
            probs = jnp.exp2((score - top[:, cols]) * exponent)
            pbuf[:, cols] = probs.astype(BF16)
            dsbuf[:, cols] = (probs * (grad_probs - delta[0:1, cols])).astype(BF16)
        grad_scores = dsbuf[...]
        value_part = jnp.dot(pbuf[...], grows[...], preferred_element_type=F32)
        key_part = jnp.dot(grad_scores, qrows[...], preferred_element_type=F32) * scaling
        part[pl.ds(chunk * 4, 4), 1] = value_part.reshape(4, SPAN, DIM)
        part[pl.ds(chunk * 4, 4), 0] = key_part.reshape(4, SPAN, DIM)
        keys_t = keys.astype(F32).T.astype(BF16)
        dqt[...] += jnp.dot(keys_t, grad_scores, preferred_element_type=F32)

        @pl.when(step == 0)
        def _():
            send_halves(base, dz, 0)
            send_halves(base, dz, 2)

        @pl.when(step == 1)
        def _():
            send_halves(base, dz, 1)
            send_halves(base, dz, 3)

        @pl.when(step == 3)
        def _():
            send_second(base, dz, 2)

        @pl.when(step == 4)
        def _():
            send_second(base, dz, 3)

        @pl.when(step == 5)
        def _():
            send_second(base, dz, 1)

        @pl.when(step == 6)
        def _():
            send_first_halves(base, dz)
            send_second(base, dz, 0)

        @pl.when(turn == 8)
        def _():
            send_first(32, 1)

        @pl.when(turn == 10)
        def _():
            await_units(reduce_recv.at[1, 4], 4)
            await_units(reduce_recv.at[1, 9], 4)
            for c in range(2):
                slot, sums = own_sum(32, 1, c)
                put(slot, sums)
                send(stage.at[slot], z_in.at[c], reduce_send, reduce_z, z_other)

        return 0

    lax.fori_loop(0, 16, backward, 0)

    send_first(0, 0)
    for s in range(2):
        for h in range(HEADS):
            here = pl.ds((s * HEADS + h) * SPAN, SPAN)
            dq_ref[pl.ds(s * SPAN, SPAN), pl.ds(h * DIM, DIM)] = (
                (dqt[:, here] * scaling).T.astype(BF16)
            )
    await_units(reduce_recv.at[0, 4], 4)
    await_units(reduce_z, 2)
    await_units(reduce_recv.at[0, 9], 4)
    for c in range(2):
        _, sums = own_sum(0, 0, c)
        rows = pl.ds(c * SPAN, SPAN)
        dk_ref[rows, :] = (sums[0] + z_in[c, 0].astype(F32)).astype(BF16)
        dv_ref[rows, :] = (sums[1] + z_in[c, 1].astype(F32)).astype(BF16)
    await_units(gather_send, 62)
    await_units(reduce_send, 62)


def local(queries, key_rows, value_slot_rows, out_grad, span_order):
    rows = queries.shape[0]
    vmem = pl.BlockSpec(memory_space=pltpu.VMEM)
    unit = (2, SPAN, DIM)
    dma = pltpu.SemaphoreType.DMA
    dq, dk, dv = pl.pallas_call(
        kernel,
        out_shape=(
            jax.ShapeDtypeStruct((rows, HEADS * DIM), BF16),
            jax.ShapeDtypeStruct((rows, DIM), BF16),
            jax.ShapeDtypeStruct((rows, DIM), BF16),
        ),
        in_specs=[
            pl.BlockSpec(memory_space=pltpu.SMEM), vmem, vmem,
            pl.BlockSpec(memory_space=pl.ANY), pl.BlockSpec(memory_space=pl.ANY),
        ],
        out_specs=(vmem, vmem, vmem),
        scratch_shapes=[
            pltpu.VMEM((64,) + unit, BF16),
            pltpu.VMEM((64,) + unit, F32),
            pltpu.VMEM((64,) + unit, BF16),
            pltpu.VMEM((64, SPAN, DIM), BF16),
            pltpu.VMEM((2, 4, 2, 2) + unit, BF16),
            pltpu.VMEM((2, 2, 2) + unit, BF16),
            pltpu.VMEM((2,) + unit, BF16),
            pltpu.VMEM((2 * DIM, COLS), BF16),
            pltpu.VMEM((DIM, COLS), BF16),
            pltpu.VMEM((COLS, DIM), BF16),
            pltpu.VMEM((COLS, DIM), BF16),
            pltpu.VMEM((2, CHUNK, 2 * DIM), BF16),
            pltpu.VMEM((CHUNK, COLS), BF16),
            pltpu.VMEM((CHUNK, COLS), BF16),
            pltpu.VMEM((DIM, COLS), F32),
            pltpu.VMEM((1, COLS), F32),
            pltpu.VMEM((8, COLS), F32),
            pltpu.VMEM((8, COLS), F32),
            pltpu.SMEM((64,), jnp.int32),
            dma((4,)), dma, dma((2, 10)), dma, dma, dma((2, 10)), dma,
        ],
        compiler_params=pltpu.CompilerParams(
            collective_id=0, has_side_effects=True, vmem_limit_bytes=60 * 1024 * 1024,
        ),
    )(
        span_order,
        queries.reshape(rows, HEADS * DIM),
        out_grad.reshape(rows, HEADS * DIM),
        key_rows.reshape(rows, DIM),
        value_slot_rows.reshape(rows, DIM),
    )
    return (
        dq.reshape(rows, HEADS, DIM),
        dk.reshape(rows, 1, DIM),
        dv.reshape(rows, 1, DIM),
    )


def solution(mesh):
    row = P(("seq", "ctx"), "tp", None)
    return jax.shard_map(
        local,
        mesh=mesh,
        in_specs=(row, row, row, row, P("seq")),
        out_specs=(row, row, row),
        check_vma=False,
    )
```

time: 611 us -> 78.5 us (0.13)
  waiting for transfers between devices: 374 us -> 0 us
  matrix products: 163 us -> 0 us
  Pallas kernels: 0 us -> 72.5 us
  local copies, waits for them, and re-layouts: 30.8 us -> 5.11 us
  other arithmetic: 23.1 us -> 0 us
  between operations: 14.1 us -> 0.65 us
    reduce_scatter x1 -> x0, waiting for transfers between devices: 258 us -> none  [sent_together(): lax.psum_scatter(both, axis, scatter_dimension=dim, tiled=True)]
    dot_general x112 -> x0, matrix products: 163 us -> none  [the longest x32 49.6 us: block_scores(): jnp.einsum('hqd,khd->hqk', query_group, keys_part, preferred_element_type...]
    all_gather x1 -> x0, waiting for transfers between devices: 116 us -> none  [in_one_piece(): lax.all_gather(both, axis, axis=dim, tiled=True)]
    pallas_call x0 -> x1, Pallas kernels: none -> 72.5 us  [local(): pl.pallas_call(kernel, out_shape=(jax.ShapeDtypeStruct((rows, HEADS * DIM...]
    while x80 -> x0, local copies, waits for them, and re-layouts: 12.9 us -> none
    reduce_sum x17 -> x0, other arithmetic: 11.3 us -> none  [the longest x16 9.93 us: forward_step(): running_sum = running_sum * rescale + jnp.sum(weights, axis=2)]
    concatenate x2 -> x0, other arithmetic: 8.76 us -> none  [the longest x1 7.22 us: sent_together(): both = jnp.concatenate(arrays, axis=along)]
  transfers between devices with their start and end apart: 2 -> 0, of which waited for: 2 -> 0; matrix products, arithmetic and copies ran while one was open for 0% -> 0% of each run, Pallas kernels for 0% -> 0%
where the time goes in v1:
time: 78.5 us; the launch traced here: 78.2 us
  Pallas kernels  72.5 us (92%)
  local copies, waits for them, and re-layouts  5.11 us (7%)
    pallas_call x1, Pallas kernels, local(): pl.pallas_call(kernel, out_shape=(jax.ShapeDtypeStruct((rows, HEADS * DIM...  72.5 us
    reshape x1, local copies, waits for them, and re-layouts, local(): out_grad.reshape(rows, HEADS * DIM)  1.87 us
    reshape x1, local copies, waits for them, and re-layouts, local(): dq.reshape(rows, HEADS, DIM)  1.75 us

profile of v1, /device:TPU:32, one launch (start us, length us, event | category | flops | bytes accessed | tf_op | source)
XLA Modules:
  0.0 78.2 jit_solution(12840373991067393118)
XLA Ops:
  0.6 1.9 %copy_bitcast_fusion = (bf16[256,512]{1,0:T(8,128)(2,1)}, bf16[256,512]{1,0:T(8,128)(2,1)}) fusion(bf16[32,8,4,128]{3,2,1,0:T(4,128)(2,1)} %bitcast.10, bf16[32,8,4,128]{3,2,1,0:T(4,128)(2,1)} %bitcast.11), kind=kLoop, calls=%fused_computation | loop fusion | bytes 1048576 | tf_op jit(solution)/shard_map/reshape | solution.py:441
  2.5 72.5 %shard_map.76 = (bf16[256,512]{1,0:T(8,128)(2,1)}, bf16[256,128]{1,0:T(8,128)(2,1)}, bf16[256,128]{1,0:T(8,128)(2,1)}) custom-call(s32[64]{0:T(128)} %span_ref.1, bf16[256,512]{1,0:T(8,128)(2,1)} %get-tuple-element.10.q_ref, bf16[256,512]{1,0:T(8,128)(2,1)} %get-tuple-element.9.g_ref, bf16[256,128]{1,0:T(8,128)(2,1)} %bitcast.12, bf16[256,128]{1,0:T(8,128)(2,1)} %bitcast.13), custom_call_target="tpu_custom_call" | custom-call | tf_op jit(solution)/shard_map/pallas_call | solution.py:401
  75.0 0.0 copy-start.1
  75.0 1.7 %reshape.31 = bf16[256,4,128]{2,1,0:T(4,128)(2,1)} reshape(bf16[256,512]{1,0:T(8,128)(2,1)} %get-tuple-element.6) | data formatting | bytes 524288 | tf_op jit(solution)/shard_map/reshape | solution.py:446
  76.7 0.0 copy-done.1
  76.7 0.0 copy-start
  76.7 0.6 copy.14
  77.4 0.2 copy-done
  77.6 0.6 copy.15
Async XLA Ops:
  75.0 1.8 %copy-start.1 = (bf16[256,128]{1,0:T(8,128)(2,1)S(1)}, bf16[256,128]{1,0:T(8,128)(2,1)}, u32[]{:S(2)}) copy-start(bf16[256,128]{1,0:T(8,128)(2,1)} %get-tuple-element.7) | copy-start | bytes 196612
  76.7 0.9 %copy-start = (bf16[256,128]{1,0:T(8,128)(2,1)S(1)}, bf16[256,128]{1,0:T(8,128)(2,1)}, u32[]{:S(2)}) copy-start(bf16[256,128]{1,0:T(8,128)(2,1)} %get-tuple-element.8) | copy-start | bytes 196612

commit v2 on v0

v2 whole, which is shorter than its diff:
```python
import math

import jax
import jax.numpy as jnp
from jax import lax
from jax.experimental import pallas as pl
from jax.experimental.pallas import tpu as pltpu
from jax.sharding import PartitionSpec as P

MESH = pl.DeviceIdType.MESH
SPAN = 128
HEADS = 4
DIM = 128
COLS = 2 * HEADS * SPAN
CHUNK = 4 * SPAN
WIDE = 256
TILES = COLS // WIDE
BLOCK = 64
HIDDEN = -1e30
F32 = jnp.float32
BF16 = jnp.bfloat16

CHUNKS = (
    ((0, 0, 0), (1, 0, 0), (0, 1, 0), (0, 3, 0)),
    ((0, 0, 1), (1, 0, 1), (1, 1, 0), (1, 3, 0)),
    ((0, 1, 1), (0, 3, 1), (1, 1, 1), (1, 3, 1)),
    ((0, 2, 0), (1, 2, 0), (0, 2, 1), (1, 2, 1)),
)
FORWARD = (
    (0, 0), (1, 0), (2, 0), (3, 0), (4, 0), (0, 1), (1, 1), (2, 1),
    (3, 1), (5, 0), (4, 1), (5, 1), (6, 0), (6, 1), (7, 0), (7, 1),
)
BACKWARD = (
    (7, 1), (7, 0), (6, 1), (6, 0), (5, 1), (5, 0), (4, 1), (4, 0),
    (3, 1), (3, 0), (2, 1), (2, 0), (1, 1), (0, 1), (1, 0), (0, 0),
)
PLACE = {unit: 4 * i + j for i, units in enumerate(CHUNKS) for j, unit in enumerate(units)}


def pick(step, values):
    return sum(jnp.where(step == i, v, 0) for i, v in enumerate(values) if v)


def when(condition):
    def run(body):
        lax.fori_loop(0, condition.astype(jnp.int32), lambda _, c: (body(), c)[1], 0)

    return run


def kernel(
    span_ref, q_ref, g_ref, k_ref, v_ref,
    dq_ref, dk_ref, dv_ref,
    kv, part, stage, half_in, x_in, e_in, z_in, dq_out, dq_in,
    qt, gt, qrows, grows, lhs, pbuf, dsbuf, dqt, top, total, delta, stats_out, stats_in,
    spans, own_spans,
    load_sem, gather_send, gather_recv, gather_z, q_send, q_recv, stat_send, stat_recv,
    reduce_send, reduce_recv, reduce_z, dq_send, dq_recv,
):
    me = lax.axis_index("ctx")
    x, z, y = me // 8, (me // 4) % 2, me % 4

    def at(xx, zz, yy):
        return (xx % 4) * 8 + (zz % 2) * 4 + yy

    x_ways = (at(x + 1, z, y), at(x + 3, z, y))
    partner = at(x, z, y + 1 - 2 * (y % 2))
    other = at(x, z, 3 - y)
    z_other = at(x, z + 1, y)

    def slot_of(base, c, da, e):
        return base + PLACE[(c, da, e)]

    loads = []
    for c in range(2):
        own = slot_of(0, c, 0, 0)
        rows = pl.ds(c * SPAN, SPAN)
        loads.append(pltpu.make_async_copy(k_ref.at[rows], kv.at[own, 0], load_sem.at[2 * c]))
        loads.append(pltpu.make_async_copy(v_ref.at[rows], kv.at[own, 1], load_sem.at[2 * c + 1]))
    loads.append(pltpu.make_async_copy(q_ref, qrows.at[0], load_sem.at[4]))
    loads.append(pltpu.make_async_copy(g_ref, grows.at[0], load_sem.at[5]))
    for copy in loads:
        copy.start()

    barrier = pltpu.get_barrier_semaphore()
    for device in (*x_ways, partner, other, z_other):
        pl.semaphore_signal(barrier, inc=1, device_id={"ctx": device}, device_id_type=MESH)
    pl.semaphore_wait(barrier, 5)
    for copy in loads:
        copy.wait()

    def send(src, dst, send_sem, recv_sem, device):
        pltpu.make_async_remote_copy(
            src_ref=src, dst_ref=dst, send_sem=send_sem, recv_sem=recv_sem,
            device_id={"ctx": device}, device_id_type=MESH,
        ).start()

    def await_units(sem, units):
        block = kv.at[pl.ds(0, units)]
        pltpu.make_async_copy(block, block, sem).wait()

    def gather(dz, group, src, dst, device):
        send(src, dst, gather_send, gather_recv.at[dz, group], device)

    def arrived(dz, *groups):
        for group in groups:
            await_units(gather_recv.at[dz, group], (1, 2, 1, 2, 1, 1, 2, 1, 2, 1)[group])

    def along_x(dz, group, c, e):
        unit = kv.at[slot_of(16 * dz, c, 0, e)]
        gather(dz, group, unit, kv.at[slot_of(16 * dz, c, 3, e)], x_ways[0])
        gather(dz, group, unit, kv.at[slot_of(16 * dz, c, 1, e)], x_ways[1])

    def opposite_x(dz, group, c, e):
        there, up, down = (slot_of(16 * dz, c, da, e) for da in (2, 3, 1))
        gather(dz, group, kv.at[up, 0], kv.at[there, 0], x_ways[0])
        gather(dz, group, kv.at[down, 1], kv.at[there, 1], x_ways[1])

    def across(dz, group, c, da):
        src, dst = slot_of(16 * dz, c, da, 0), slot_of(16 * dz, c, da, 1)
        gather(dz, group, kv.at[src], kv.at[dst], other)

    def gather_own(dz):
        along_x(dz, 1, 0, 0)
        across(dz, 0, 0, 0)
        along_x(dz, 8, 1, 0)
        across(dz, 5, 1, 0)

    def gather_a(dz):
        arrived(dz, 1)
        opposite_x(dz, 2, 0, 0)
        arrived(dz, 0)
        along_x(dz, 3, 0, 1)

    def gather_b(dz):
        arrived(dz, 8)
        opposite_x(dz, 9, 1, 0)
        across(dz, 6, 1, 1)
        across(dz, 6, 1, 3)

    def gather_c(dz):
        arrived(dz, 9)
        across(dz, 7, 1, 2)
        arrived(dz, 3)
        opposite_x(dz, 4, 0, 1)

    for c in range(2):
        send(
            kv.at[slot_of(0, c, 0, 0)], kv.at[slot_of(16, c, 0, 0)],
            gather_send, gather_z, z_other,
        )
    gather_own(0)
    send(qrows.at[0], qrows.at[1], q_send, q_recv, partner)
    send(grows.at[0], grows.at[1], q_send, q_recv, partner)

    for dz in range(2):
        for c, da, e in PLACE:
            owner = at(x + da, z + dz, y if e == 0 else 3 - y)
            spans[slot_of(16 * dz, c, da, e)] = span_ref[owner * 2 + c]
    for group, device in enumerate((me, partner)):
        for s in range(2):
            own_spans[group * 2 + s] = span_ref[device * 2 + s]

    lane = lax.broadcasted_iota(jnp.int32, (SPAN, SPAN), 1)
    sublane = lax.broadcasted_iota(jnp.int32, (SPAN, SPAN), 0)

    def prepare(group):
        for block in range(COLS // SPAN):
            here = pl.ds(block * SPAN, SPAN)
            qt[group, 0:DIM, here] = qrows[group, here, :].astype(F32).T.astype(BF16)
            gt[group, :, here] = grows[group, here, :].astype(F32).T.astype(BF16)
            row = block % HEADS * (SPAN // HEADS) + lane // HEADS
            qt[group, DIM : 2 * DIM, here] = jnp.where(row == sublane, 1.0, 0.0).astype(BF16)

    prepare(0)
    top[...] = jnp.full_like(top, HIDDEN)
    total[...] = jnp.zeros_like(total)
    delta[...] = jnp.zeros_like(delta)
    dqt[...] = jnp.zeros_like(dqt)

    exponent = math.log2(math.e) / math.sqrt(DIM)
    scaling = 1.0 / math.sqrt(DIM)

    def masked_keys(chunk, keys, group):
        ahead = sublane - lane
        for s in range(2):
            lhs[s, :, 0:DIM] = keys
            for u in range(4):
                limit = (own_spans[group * 2 + s] - spans[chunk * 4 + u]) * SPAN
                lhs[s, u * SPAN : (u + 1) * SPAN, DIM : 2 * DIM] = jnp.where(
                    ahead > limit, HIDDEN, 0.0
                ).astype(BF16)

    def load_chunk(chunk):
        keys = kv[pl.ds(chunk * 4, 4), 0].reshape(CHUNK, DIM)
        values = kv[pl.ds(chunk * 4, 4), 1].reshape(CHUNK, DIM)
        return keys, values

    def fold(values, op):
        return op(values.reshape(values.shape[0] // 8, 8, WIDE), axis=0)

    def partials(group):
        stats_out[group, :, 0:COLS] = top[group]
        stats_out[group, :, COLS : 2 * COLS] = jnp.sum(total[group], axis=0, keepdims=True)
        stats_out[group, :, 2 * COLS :] = jnp.sum(delta[group], axis=0, keepdims=True)
        send(
            stats_out.at[group], stats_in.at[1 - group],
            stat_send.at[group], stat_recv.at[1 - group], partner,
        )

    def combine(group):
        here, there = stats_out.at[group], stats_in.at[group]
        pltpu.make_async_copy(there, there, stat_recv.at[group]).wait()
        first, second, third = (pl.ds(i * COLS, COLS) for i in range(3))
        highest = jnp.maximum(here[:, first], there[:, first])
        a = jnp.exp2((here[:, first] - highest) * exponent)
        b = jnp.exp2((there[:, first] - highest) * exponent)
        weight = here[:, second] * a + there[:, second] * b
        top[group] = highest + jnp.log(weight) * math.sqrt(DIM)
        delta[group, 0:1, :] = (here[:, third] * a + there[:, third] * b) / weight

    def tile_of(tile):
        return pl.ds(tile * WIDE, WIDE), tile * WIDE // (HEADS * SPAN)

    def scores(group, tile):
        cols, s = tile_of(tile)
        return jnp.dot(lhs[s], qt[group, :, cols], preferred_element_type=F32)

    def forward(step, _):
        chunk = pick(step, [c for c, _ in FORWARD])
        group = pick(step, [g for _, g in FORWARD])

        @when(step == 0)
        def _():
            gather_a(0)

        @when(step == 1)
        def _():
            gather_b(0)
            arrived(0, 5)

        @when(step == 2)
        def _():
            gather_c(0)
            await_units(gather_z, 2)
            gather_own(1)
            arrived(0, 6)

        @when(step == 3)
        def _():
            arrived(0, 2, 4, 7)

        @when(step == 4)
        def _():
            gather_a(1)

        @when(step == 5)
        def _():
            await_units(q_recv, 8)
            prepare(1)

        @when(step == 6)
        def _():
            gather_b(1)

        @when(step == 9)
        def _():
            gather_c(1)
            arrived(1, 5)

        @when(step == 12)
        def _():
            arrived(1, 6)

        @when(step == 14)
        def _():
            arrived(1, 2, 4, 7)

        @when(step == 15)
        def _():
            partials(0)

        keys, values = load_chunk(chunk)

        def grads(tile):
            cols, _ = tile_of(tile)
            return jnp.dot(values, gt[group, :, cols], preferred_element_type=F32)

        def topped(tile):
            cols, _ = tile_of(tile)
            score = scores(group, tile)
            before = top[group, :, cols]
            now = jnp.maximum(before, jnp.max(fold(score, jnp.max), axis=0, keepdims=True))
            top[group, :, cols] = now
            return score, now, jnp.exp2((before - now) * exponent)

        masked_keys(chunk, keys, group)
        ahead = topped(0)
        for tile in range(TILES):
            cols, _ = tile_of(tile)
            score, now, rescale = ahead
            if tile + 1 < TILES:
                ahead = topped(tile + 1)
            grad_probs = grads(tile)
            weight = total[group, :, cols] * rescale
            product = delta[group, :, cols] * rescale
            for row in range(0, CHUNK, BLOCK):
                weights = jnp.exp2((score[row : row + BLOCK] - now) * exponent)
                weight += fold(weights, jnp.sum)
                product += fold(weights * grad_probs[row : row + BLOCK], jnp.sum)
            total[group, :, cols] = weight
            delta[group, :, cols] = product
        return 0

    lax.fori_loop(0, 16, forward, 0)
    partials(1)
    combine(1)

    def reduce(dz, group, src, dst, device):
        send(src, dst, reduce_send, reduce_recv.at[dz, group], device)

    def put(slot, sums):
        stage[slot, 0] = sums[0].astype(BF16)
        stage[slot, 1] = sums[1].astype(BF16)

    def partial_of(slot):
        return [part[slot, 0], part[slot, 1]]

    def plus(sums, ref):
        return [sums[i] + ref[i].astype(F32) for i in range(2)]

    def plus_half(sums, slot, which):
        arrived = half_in[slot].astype(F32)
        return [sums[0] + arrived, sums[1]] if which == 0 else [sums[0], sums[1] + arrived]

    def halves(base, dz, group, c, e, sums):
        slot = slot_of(base, c, 2, e)
        put(slot, sums)
        reduce(dz, group, stage.at[slot, 0], half_in.at[slot_of(base, c, 1, e)], x_ways[0])
        reduce(dz, group, stage.at[slot, 1], half_in.at[slot_of(base, c, 3, e)], x_ways[1])

    def sum_along_x(base, dz, group, c, e, kind, way, sums):
        slot = slot_of(base, c, (1, 3)[way], e)
        put(slot, plus_half(sums, slot, way))
        reduce(dz, group, stage.at[slot], x_in.at[dz, kind, way], x_ways[way])

    def sum_across(base, dz, group, c, da, place, sums):
        slot = slot_of(base, c, da, 1)
        put(slot, sums)
        reduce(dz, group, stage.at[slot], e_in.at[dz, place], other)

    def landed(dz, *groups):
        for group in groups:
            await_units(reduce_recv.at[dz, group], (1, 1, 2, 2, 1, 2, 2, 1, 1, 1)[group])

    def reduce_d(dz):
        base = 16 * dz
        halves(base, dz, 9, 0, 0, partial_of(slot_of(base, 0, 2, 0)))
        halves(base, dz, 0, 0, 1, partial_of(slot_of(base, 0, 2, 1)))
        sum_across(base, dz, 1, 1, 2, 2, partial_of(slot_of(base, 1, 2, 1)))

    def reduce_c(dz):
        base = 16 * dz
        for da in (1, 3):
            sum_across(base, dz, 3, 1, da, da, partial_of(slot_of(base, 1, da, 1)))
        landed(dz, 0)
        for way, da in enumerate((1, 3)):
            sum_along_x(base, dz, 2, 0, 1, 1, way, partial_of(slot_of(base, 0, da, 1)))

    def reduce_c_opposite(dz):
        base = 16 * dz
        landed(dz, 1)
        halves(base, dz, 4, 1, 0, plus(partial_of(slot_of(base, 1, 2, 0)), e_in.at[dz, 2]))

    def reduce_b(dz):
        base = 16 * dz
        sum_across(base, dz, 8, 1, 0, 0, partial_of(slot_of(base, 1, 0, 1)))
        landed(dz, 2)
        sums = partial_of(slot_of(base, 0, 0, 1))
        for way in range(2):
            sums = plus(sums, x_in.at[dz, 1, way])
        sum_across(base, dz, 7, 0, 0, 4, sums)
        landed(dz, 3, 4)
        for way, da in enumerate((1, 3)):
            sums = plus(partial_of(slot_of(base, 1, da, 0)), e_in.at[dz, da])
            sum_along_x(base, dz, 6, 1, 0, 2, way, sums)

    def reduce_a(dz):
        base = 16 * dz
        landed(dz, 9)
        for way, da in enumerate((1, 3)):
            sum_along_x(base, dz, 5, 0, 0, 0, way, partial_of(slot_of(base, 0, da, 0)))

    def own_sums(dz):
        landed(dz, 7, 8, 6, 5)
        for c in range(2):
            slot = slot_of(16 * dz, c, 0, 0)
            sums = partial_of(slot)
            for way in range(2):
                sums = plus(sums, x_in.at[dz, 2 * c, way])
            yield c, slot, plus(sums, e_in.at[dz, 4 - 4 * c])

    def query_grads(group):
        for block in range(COLS // SPAN):
            here = pl.ds(block * SPAN, SPAN)
            yield here, (dqt[group, :, here] * scaling).T

    def backward(step, _):
        chunk = pick(step, [c for c, _ in BACKWARD])
        group = pick(step, [g for _, g in BACKWARD])

        @when(step == 1)
        def _():
            combine(0)

        keys, values = load_chunk(chunk)
        masked_keys(chunk, keys, group)
        for tile in range(TILES):
            cols, _ = tile_of(tile)
            score = scores(group, tile)
            grad_probs = jnp.dot(values, gt[group, :, cols], preferred_element_type=F32)
            lse, mean = top[group, :, cols], delta[group, 0:1, cols]
            for row in range(0, CHUNK, BLOCK):
                rows = slice(row, row + BLOCK)
                probs = jnp.exp2((score[rows] - lse) * exponent)
                pbuf[rows, cols] = probs.astype(BF16)
                dsbuf[rows, cols] = (probs * (grad_probs[rows] - mean)).astype(BF16)
        units = pl.ds(chunk * 4, 4)
        value_part = jnp.dot(pbuf[...], grows[group], preferred_element_type=F32)
        key_part = jnp.dot(dsbuf[...], qrows[group], preferred_element_type=F32) * scaling
        for which, found in ((1, value_part), (0, key_part)):
            before = jnp.where(group == 1, 0.0, part[units, which])
            part[units, which] = before + found.reshape(4, SPAN, DIM)
        keys_t = keys.astype(F32).T.astype(BF16)
        dqt[group] += jnp.dot(keys_t, dsbuf[...], preferred_element_type=F32)

        events = (
            (1, 9, reduce_d), (3, 11, reduce_c), (4, 12, reduce_c_opposite), (6, 14, reduce_b),
        )
        for early, late, event in events:

            @when((step == early) | (step == late))
            def _():
                event(jnp.where(step < 8, 1, 0))

        @when(step == 7)
        def _():
            reduce_a(1)

        @when(step == 10)
        def _():
            for c, slot, sums in own_sums(1):
                put(slot, sums)
                send(stage.at[slot], z_in.at[c], reduce_send, reduce_z, z_other)

        @when(step == 13)
        def _():
            for here, block in query_grads(1):
                dq_out[here, :] = block.astype(BF16)
            send(dq_out, dq_in, dq_send, dq_recv, partner)

        return 0

    lax.fori_loop(0, 16, backward, 0)
    reduce_a(0)
    await_units(reduce_z, 2)
    for c, _, sums in own_sums(0):
        rows = pl.ds(c * SPAN, SPAN)
        dk_ref[rows, :] = (sums[0] + z_in[c, 0].astype(F32)).astype(BF16)
        dv_ref[rows, :] = (sums[1] + z_in[c, 1].astype(F32)).astype(BF16)
    await_units(dq_recv, 4)
    for here, block in query_grads(0):
        dq_ref[here, :] = (block + dq_in[here, :].astype(F32)).astype(BF16)
    await_units(gather_send, 30)
    await_units(q_send, 8)
    await_units(reduce_send, 30)
    await_units(dq_send, 4)
    for group in range(2):
        sent = stats_out.at[group]
        pltpu.make_async_copy(sent, sent, stat_send.at[group]).wait()


def local(queries, key_rows, value_slot_rows, out_grad, span_order):
    rows = queries.shape[0]
    vmem = pl.BlockSpec(memory_space=pltpu.VMEM)
    unit = (2, SPAN, DIM)
    dma = pltpu.SemaphoreType.DMA
    dq, dk, dv = pl.pallas_call(
        kernel,
        out_shape=(
            jax.ShapeDtypeStruct((rows * HEADS, DIM), BF16),
            jax.ShapeDtypeStruct((rows, DIM), BF16),
            jax.ShapeDtypeStruct((rows, DIM), BF16),
        ),
        in_specs=[
            pl.BlockSpec(memory_space=pltpu.SMEM),
            *([pl.BlockSpec(memory_space=pl.ANY)] * 4),
        ],
        out_specs=(vmem, vmem, vmem),
        scratch_shapes=[
            pltpu.VMEM((32,) + unit, BF16),
            pltpu.VMEM((32,) + unit, F32),
            pltpu.VMEM((32,) + unit, BF16),
            pltpu.VMEM((32, SPAN, DIM), BF16),
            pltpu.VMEM((2, 3, 2) + unit, BF16),
            pltpu.VMEM((2, 5) + unit, BF16),
            pltpu.VMEM((2,) + unit, BF16),
            pltpu.VMEM((COLS, DIM), BF16),
            pltpu.VMEM((COLS, DIM), BF16),
            pltpu.VMEM((2, 2 * DIM, COLS), BF16),
            pltpu.VMEM((2, DIM, COLS), BF16),
            pltpu.VMEM((2, COLS, DIM), BF16),
            pltpu.VMEM((2, COLS, DIM), BF16),
            pltpu.VMEM((2, CHUNK, 2 * DIM), BF16),
            pltpu.VMEM((CHUNK, COLS), BF16),
            pltpu.VMEM((CHUNK, COLS), BF16),
            pltpu.VMEM((2, DIM, COLS), F32),
            pltpu.VMEM((2, 1, COLS), F32),
            pltpu.VMEM((2, 8, COLS), F32),
            pltpu.VMEM((2, 8, COLS), F32),
            pltpu.VMEM((2, 1, 3 * COLS), F32),
            pltpu.VMEM((2, 1, 3 * COLS), F32),
            pltpu.SMEM((32,), jnp.int32),
            pltpu.SMEM((4,), jnp.int32),
            dma((6,)), dma, dma((2, 10)), dma, dma, dma, dma((2,)), dma((2,)),
            dma, dma((2, 10)), dma, dma, dma,
        ],
        compiler_params=pltpu.CompilerParams(
            collective_id=0, has_side_effects=True, vmem_limit_bytes=60 * 1024 * 1024,
        ),
    )(
        span_order,
        queries.reshape(rows * HEADS, DIM),
        out_grad.reshape(rows * HEADS, DIM),
        key_rows.reshape(rows, DIM),
        value_slot_rows.reshape(rows, DIM),
    )
    return (
        dq.reshape(rows, HEADS, DIM),
        dk.reshape(rows, 1, DIM),
        dv.reshape(rows, 1, DIM),
    )


def solution(mesh):
    row = P(("seq", "ctx"), "tp", None)
    return jax.shard_map(
        local,
        mesh=mesh,
        in_specs=(row, row, row, row, P("seq")),
        out_specs=(row, row, row),
        check_vma=False,
    )
```

time: 611 us -> 73.5 us (0.12)
  waiting for transfers between devices: 374 us -> 0 us
  matrix products: 163 us -> 0 us
  Pallas kernels: 0 us -> 68.9 us
  local copies, waits for them, and re-layouts: 30.8 us -> 3.27 us
  other arithmetic: 23.1 us -> 0 us
  between operations: 14.1 us -> 0.65 us
    reduce_scatter x1 -> x0, waiting for transfers between devices: 258 us -> none  [sent_together(): lax.psum_scatter(both, axis, scatter_dimension=dim, tiled=True)]
    dot_general x112 -> x0, matrix products: 163 us -> none  [the longest x32 49.6 us: block_scores(): jnp.einsum('hqd,khd->hqk', query_group, keys_part, preferred_element_type...]
    all_gather x1 -> x0, waiting for transfers between devices: 116 us -> none  [in_one_piece(): lax.all_gather(both, axis, axis=dim, tiled=True)]
    pallas_call x0 -> x1, Pallas kernels: none -> 68.9 us  [local(): pl.pallas_call(kernel, out_shape=(jax.ShapeDtypeStruct((rows * HEADS, DIM...]
    while x80 -> x0, local copies, waits for them, and re-layouts: 12.9 us -> none
    reduce_sum x17 -> x0, other arithmetic: 11.3 us -> none  [the longest x16 9.93 us: forward_step(): running_sum = running_sum * rescale + jnp.sum(weights, axis=2)]
    concatenate x2 -> x0, other arithmetic: 8.76 us -> none  [the longest x1 7.22 us: sent_together(): both = jnp.concatenate(arrays, axis=along)]
  transfers between devices with their start and end apart: 2 -> 0, of which waited for: 2 -> 0; matrix products, arithmetic and copies ran while one was open for 0% -> 0% of each run, Pallas kernels for 0% -> 0%
where the time goes in v2:
time: 73.5 us; the launch traced here: 72.8 us
  Pallas kernels  68.9 us (94%)
  local copies, waits for them, and re-layouts  3.27 us (4%)
    pallas_call x1, Pallas kernels, local(): pl.pallas_call(kernel, out_shape=(jax.ShapeDtypeStruct((rows * HEADS, DIM...  68.9 us
    unnamed x7, local copies, waits for them, and re-layouts  3.27 us

profile of v2, /device:TPU:32, one launch (start us, length us, event | category | flops | bytes accessed | tf_op | source)
XLA Modules:
  0.0 72.8 jit_solution(3431022748468992264)
XLA Ops:
  0.6 68.9 %shard_map.76 = (bf16[1024,128]{1,0:T(8,128)(2,1)}, bf16[256,128]{1,0:T(8,128)(2,1)}, bf16[256,128]{1,0:T(8,128)(2,1)}) custom-call(s32[64]{0:T(128)} %span_ref.1, bf16[1024,128]{1,0:T(8,128)(2,1)} %bitcast.7, bf16[1024,128]{1,0:T(8,128)(2,1)} %bitcast.8, bf16[256,128]{1,0:T(8,128)(2,1)} %bitcast.10, bf16[256,128]{1,0:T(8,128)(2,1)} %bitcast.11), custom_call_target="tpu_custom_call" | custom-call | tf_op jit(solution)/shard_map/pallas_call | solution.py:488
  69.5 0.0 copy-start.1
  69.5 1.8 %copy.11 = bf16[256,4,128]{2,1,0:T(4,128)(2,1)} copy(bf16[256,4,128]{2,1,0:T(4,128)(2,1)} %bitcast.9) | data formatting | bytes 524288
  71.3 0.0 copy-done.1
  71.3 0.0 copy-start
  71.3 0.6 copy.12
  71.9 0.2 copy-done
  72.2 0.6 copy.13
Async XLA Ops:
  69.5 1.8 %copy-start.1 = (bf16[256,128]{1,0:T(8,128)(2,1)S(1)}, bf16[256,128]{1,0:T(8,128)(2,1)}, u32[]{:S(2)}) copy-start(bf16[256,128]{1,0:T(8,128)(2,1)} %get-tuple-element.7) | copy-start | bytes 196612
  71.3 0.9 %copy-start = (bf16[256,128]{1,0:T(8,128)(2,1)S(1)}, bf16[256,128]{1,0:T(8,128)(2,1)}, u32[]{:S(2)}) copy-start(bf16[256,128]{1,0:T(8,128)(2,1)} %get-tuple-element.8) | copy-start | bytes 196612

commit v3 on v2

--- a/solution.py
+++ b/solution.py
@@ -28,7 +28,7 @@
 )
 FORWARD = (
     (0, 0), (1, 0), (2, 0), (3, 0), (4, 0), (0, 1), (1, 1), (2, 1),
-    (3, 1), (5, 0), (4, 1), (5, 1), (6, 0), (6, 1), (7, 0), (7, 1),
+    (3, 1), (5, 0), (4, 1), (5, 1), (6, 0), (7, 0), (6, 1), (7, 1),
 )
 BACKWARD = (
     (7, 1), (7, 0), (6, 1), (6, 0), (5, 1), (5, 0), (4, 1), (4, 0),
@@ -52,7 +52,7 @@
     span_ref, q_ref, g_ref, k_ref, v_ref,
     dq_ref, dk_ref, dv_ref,
     kv, part, stage, half_in, x_in, e_in, z_in, dq_out, dq_in,
-    qt, gt, qrows, grows, lhs, pbuf, dsbuf, dqt, top, total, delta, stats_out, stats_in,
+    qt, gt, qrows, grows, lhs, sbuf, pbuf, dsbuf, dqt, top, total, delta, stats_out, stats_in,
     spans, own_spans,
     load_sem, gather_send, gather_recv, gather_z, q_send, q_recv, stat_send, stat_recv,
     reduce_send, reduce_recv, reduce_z, dq_send, dq_recv,
@@ -86,7 +86,7 @@
     for device in (*x_ways, partner, other, z_other):
         pl.semaphore_signal(barrier, inc=1, device_id={"ctx": device}, device_id_type=MESH)
     pl.semaphore_wait(barrier, 5)
-    for copy in loads:
+    for copy in loads[:4]:
         copy.wait()
 
     def send(src, dst, send_sem, recv_sem, device):
@@ -150,6 +150,8 @@
             gather_send, gather_z, z_other,
         )
     gather_own(0)
+    for copy in loads[4:]:
+        copy.wait()
     send(qrows.at[0], qrows.at[1], q_send, q_recv, partner)
     send(grows.at[0], grows.at[1], q_send, q_recv, partner)
 
@@ -219,93 +221,92 @@
         top[group] = highest + jnp.log(weight) * math.sqrt(DIM)
         delta[group, 0:1, :] = (here[:, third] * a + there[:, third] * b) / weight
 
-    def tile_of(tile):
-        return pl.ds(tile * WIDE, WIDE), tile * WIDE // (HEADS * SPAN)
-
-    def scores(group, tile):
-        cols, s = tile_of(tile)
-        return jnp.dot(lhs[s], qt[group, :, cols], preferred_element_type=F32)
-
     def forward(step, _):
         chunk = pick(step, [c for c, _ in FORWARD])
         group = pick(step, [g for _, g in FORWARD])
 
-        @when(step == 0)
-        def _():
-            gather_a(0)
-
-        @when(step == 1)
-        def _():
-            gather_b(0)
-            arrived(0, 5)
-
-        @when(step == 2)
-        def _():
-            gather_c(0)
-            await_units(gather_z, 2)
-            gather_own(1)
-            arrived(0, 6)
-
-        @when(step == 3)
-        def _():
-            arrived(0, 2, 4, 7)
-
-        @when(step == 4)
-        def _():
-            gather_a(1)
-
-        @when(step == 5)
-        def _():
-            await_units(q_recv, 8)
-            prepare(1)
-
-        @when(step == 6)
-        def _():
-            gather_b(1)
-
-        @when(step == 9)
-        def _():
-            gather_c(1)
-            arrived(1, 5)
-
-        @when(step == 12)
-        def _():
-            arrived(1, 6)
-
-        @when(step == 14)
-        def _():
-            arrived(1, 2, 4, 7)
-
-        @when(step == 15)
-        def _():
-            partials(0)
+        @when(step < 4)
+        def _():
+            @when(step == 0)
+            def _():
+                gather_a(0)
+
+            @when(step == 1)
+            def _():
+                gather_b(0)
+                arrived(0, 5)
+
+            @when(step == 2)
+            def _():
+                gather_c(0)
+                await_units(gather_z, 2)
+                gather_own(1)
+                arrived(0, 6)
+
+            @when(step == 3)
+            def _():
+                arrived(0, 2, 4, 7)
+
+        @when((step >= 4) & (step < 6))
+        def _():
+            @when(step == 4)
+            def _():
+                gather_a(1)
+
+            @when(step == 5)
+            def _():
+                gather_b(1)
+                await_units(q_recv, 8)
+                prepare(1)
+
+        @when(step >= 8)
+        def _():
+            @when(step == 8)
+            def _():
+                gather_c(1)
+                arrived(1, 5)
+
+            @when(step == 12)
+            def _():
+                arrived(1, 6)
+
+            @when(step == 13)
+            def _():
+                arrived(1, 2, 4, 7)
+
+            @when(step == 14)
+            def _():
+                partials(0)
 
         keys, values = load_chunk(chunk)
 
         def grads(tile):
-            cols, _ = tile_of(tile)
+            cols = pl.ds(tile * WIDE, WIDE)
             return jnp.dot(values, gt[group, :, cols], preferred_element_type=F32)
 
         def topped(tile):
-            cols, _ = tile_of(tile)
-            score = scores(group, tile)
+            cols = pl.ds(tile * WIDE, WIDE)
+            s = tile * WIDE // (HEADS * SPAN)
+            score = jnp.dot(lhs[s], qt[group, :, cols], preferred_element_type=F32)
+            sbuf[chunk * 2 + group, :, cols] = score
             before = top[group, :, cols]
             now = jnp.maximum(before, jnp.max(fold(score, jnp.max), axis=0, keepdims=True))
             top[group, :, cols] = now
-            return score, now, jnp.exp2((before - now) * exponent)
+            return now, jnp.exp2((before - now) * exponent)
 
         masked_keys(chunk, keys, group)
         ahead = topped(0)
         for tile in range(TILES):
-            cols, _ = tile_of(tile)
-            score, now, rescale = ahead
+            cols = pl.ds(tile * WIDE, WIDE)
+            now, rescale = ahead
             if tile + 1 < TILES:
                 ahead = topped(tile + 1)
             grad_probs = grads(tile)
             weight = total[group, :, cols] * rescale
             product = delta[group, :, cols] * rescale
             for row in range(0, CHUNK, BLOCK):
-                weights = jnp.exp2((score[row : row + BLOCK] - now) * exponent)
+                score = sbuf[chunk * 2 + group, row : row + BLOCK, cols]
+                weights = jnp.exp2((score - now) * exponent)
                 weight += fold(weights, jnp.sum)
                 product += fold(weights * grad_probs[row : row + BLOCK], jnp.sum)
             total[group, :, cols] = weight
@@ -355,9 +356,9 @@
 
     def reduce_d(dz):
         base = 16 * dz
+        sum_across(base, dz, 1, 1, 2, 2, partial_of(slot_of(base, 1, 2, 1)))
+        halves(base, dz, 0, 0, 1, partial_of(slot_of(base, 0, 2, 1)))
         halves(base, dz, 9, 0, 0, partial_of(slot_of(base, 0, 2, 0)))
-        halves(base, dz, 0, 0, 1, partial_of(slot_of(base, 0, 2, 1)))
-        sum_across(base, dz, 1, 1, 2, 2, partial_of(slot_of(base, 1, 2, 1)))
 
     def reduce_c(dz):
         base = 16 * dz
@@ -380,6 +381,9 @@
         for way in range(2):
             sums = plus(sums, x_in.at[dz, 1, way])
         sum_across(base, dz, 7, 0, 0, 4, sums)
+
+    def reduce_b_along(dz):
+        base = 16 * dz
         landed(dz, 3, 4)
         for way, da in enumerate((1, 3)):
             sums = plus(partial_of(slot_of(base, 1, da, 0)), e_in.at[dz, da])
@@ -409,20 +413,19 @@
         chunk = pick(step, [c for c, _ in BACKWARD])
         group = pick(step, [g for _, g in BACKWARD])
 
-        @when(step == 1)
+        @pl.when(step == 1)
         def _():
             combine(0)
 
         keys, values = load_chunk(chunk)
-        masked_keys(chunk, keys, group)
         for tile in range(TILES):
-            cols, _ = tile_of(tile)
-            score = scores(group, tile)
+            cols = pl.ds(tile * WIDE, WIDE)
             grad_probs = jnp.dot(values, gt[group, :, cols], preferred_element_type=F32)
             lse, mean = top[group, :, cols], delta[group, 0:1, cols]
             for row in range(0, CHUNK, BLOCK):
                 rows = slice(row, row + BLOCK)
-                probs = jnp.exp2((score[rows] - lse) * exponent)
+                score = sbuf[chunk * 2 + group, rows, cols]
+                probs = jnp.exp2((score - lse) * exponent)
                 pbuf[rows, cols] = probs.astype(BF16)
                 dsbuf[rows, cols] = (probs * (grad_probs[rows] - mean)).astype(BF16)
         units = pl.ds(chunk * 4, 4)
@@ -436,24 +439,25 @@
 
         events = (
             (1, 9, reduce_d), (3, 11, reduce_c), (4, 12, reduce_c_opposite), (6, 14, reduce_b),
+            (7, 14, reduce_b_along),
         )
         for early, late, event in events:
 
-            @when((step == early) | (step == late))
+            @pl.when((step == early) | (step == late))
             def _():
                 event(jnp.where(step < 8, 1, 0))
 
-        @when(step == 7)
+        @pl.when(step == 7)
         def _():
             reduce_a(1)
 
-        @when(step == 10)
+        @pl.when(step == 10)
         def _():
             for c, slot, sums in own_sums(1):
                 put(slot, sums)
                 send(stage.at[slot], z_in.at[c], reduce_send, reduce_z, z_other)
 
-        @when(step == 13)
+        @pl.when(step == 13)
         def _():
             for here, block in query_grads(1):
                 dq_out[here, :] = block.astype(BF16)
@@ -478,6 +482,40 @@
     for group in range(2):
         sent = stats_out.at[group]
         pltpu.make_async_copy(sent, sent, stat_send.at[group]).wait()
+
+
+def settle(*refs):
+    count = (len(refs) - 2) // 3
+    sources, targets, held = (refs[i * count : (i + 1) * count] for i in range(3))
+    in_sem, out_sem = refs[-2:]
+    copies = []
+    for i, (source, target, buffer) in enumerate(zip(sources, targets, held)):
+        copies.append((
+            pltpu.make_async_copy(source, buffer, in_sem.at[i]),
+            pltpu.make_async_copy(buffer, target, out_sem.at[i]),
+        ))
+    for inward, _ in copies:
+        inward.start()
+    for inward, outward in copies:
+        inward.wait()
+        outward.start()
+    for _, outward in copies:
+        outward.wait()
+
+
+def settled(*results):
+    anywhere = [pl.BlockSpec(memory_space=pl.ANY)] * len(results)
+    return pl.pallas_call(
+        settle,
+        out_shape=tuple(jax.ShapeDtypeStruct(r.shape, r.dtype) for r in results),
+        in_specs=anywhere,
+        out_specs=tuple(anywhere),
+        scratch_shapes=[
+            *(pltpu.VMEM(r.shape, r.dtype) for r in results),
+            pltpu.SemaphoreType.DMA((len(results),)),
+            pltpu.SemaphoreType.DMA((len(results),)),
+        ],
+    )(*results)
 
 
 def local(queries, key_rows, value_slot_rows, out_grad, span_order):
@@ -512,6 +550,7 @@
             pltpu.VMEM((2, COLS, DIM), BF16),
             pltpu.VMEM((2, COLS, DIM), BF16),
             pltpu.VMEM((2, CHUNK, 2 * DIM), BF16),
+            pltpu.VMEM((16, CHUNK, COLS), F32),
             pltpu.VMEM((CHUNK, COLS), BF16),
             pltpu.VMEM((CHUNK, COLS), BF16),
             pltpu.VMEM((2, DIM, COLS), F32),
@@ -535,6 +574,7 @@
         key_rows.reshape(rows, DIM),
         value_slot_rows.reshape(rows, DIM),
     )
+    dq, dk, dv = settled(dq, dk, dv)
     return (
         dq.reshape(rows, HEADS, DIM),
         dk.reshape(rows, 1, DIM),

time: 73.5 us -> 68.3 us (0.929)
  local copies, waits for them, and re-layouts: 3.27 us -> 0 us
  Pallas kernels: 68.9 us -> 67.5 us
    unnamed x7 -> x0, local copies, waits for them, and re-layouts: 3.27 us -> none
    pallas_call x1, Pallas kernels: 68.9 us -> 65.8 us  [local(): pl.pallas_call(kernel, out_shape=(jax.ShapeDtypeStruct((rows * HEADS, DIM...]
    pallas_call x0 -> x1, Pallas kernels: none -> 1.74 us  [settled(): pl.pallas_call(settle, out_shape=tuple((jax.ShapeDtypeStruct(r.shape, r.d...]
where the time goes in v3:
time: 68.3 us; the launch traced here: 68.1 us
  Pallas kernels  67.5 us (99%)
    pallas_call x1, Pallas kernels, local(): pl.pallas_call(kernel, out_shape=(jax.ShapeDtypeStruct((rows * HEADS, DIM...  65.8 us
    pallas_call x1, Pallas kernels, settled(): pl.pallas_call(settle, out_shape=tuple((jax.ShapeDtypeStruct(r.shape, r.d...  1.74 us

profile of v3, /device:TPU:32, one launch (start us, length us, event | category | flops | bytes accessed | tf_op | source)
XLA Modules:
  0.0 68.1 jit_solution(4510592596950496150)
XLA Ops:
  0.6 65.8 %shard_map.76 = (bf16[1024,128]{1,0:T(8,128)(2,1)}, bf16[256,128]{1,0:T(8,128)(2,1)}, bf16[256,128]{1,0:T(8,128)(2,1)}) custom-call(s32[64]{0:T(128)} %span_ref.1, bf16[1024,128]{1,0:T(8,128)(2,1)} %bitcast.7, bf16[1024,128]{1,0:T(8,128)(2,1)} %bitcast.8, bf16[256,128]{1,0:T(8,128)(2,1)} %bitcast.9, bf16[256,128]{1,0:T(8,128)(2,1)} %bitcast.10), custom_call_target="tpu_custom_call" | custom-call | tf_op jit(solution)/shard_map/pallas_call | solution.py:526
  66.4 1.7 %shard_map.77 = (bf16[1024,128]{1,0:T(8,128)(2,1)}, bf16[256,128]{1,0:T(8,128)(2,1)}, bf16[256,128]{1,0:T(8,128)(2,1)}) custom-call(bf16[1024,128]{1,0:T(8,128)(2,1)} %get-tuple-element.9.refs_0_, bf16[256,128]{1,0:T(8,128)(2,1)} %get-tuple-element.10.refs_1_, bf16[256,128]{1,0:T(8,128)(2,1)} %get-tuple-element.11.refs_2_), custom_call_target="tpu_custom_call" | custom-call | tf_op jit(solution)/shard_map/pallas_call | solution.py:508

commit v4 on v3

--- a/solution.py
+++ b/solution.py
@@ -52,7 +52,7 @@
     span_ref, q_ref, g_ref, k_ref, v_ref,
     dq_ref, dk_ref, dv_ref,
     kv, part, stage, half_in, x_in, e_in, z_in, dq_out, dq_in,
-    qt, gt, qrows, grows, lhs, sbuf, pbuf, dsbuf, dqt, top, total, delta, stats_out, stats_in,
+    qt, gt, qrows, grows, masks, sbuf, pbuf, dsbuf, dqt, top, total, delta, stats_out, stats_in,
     spans, own_spans,
     load_sem, gather_send, gather_recv, gather_z, q_send, q_recv, stat_send, stat_recv,
     reduce_send, reduce_recv, reduce_z, dq_send, dq_recv,
@@ -183,15 +183,18 @@
     exponent = math.log2(math.e) / math.sqrt(DIM)
     scaling = 1.0 / math.sqrt(DIM)
 
-    def masked_keys(chunk, keys, group):
+    def mask_step(place, _):
+        chunk, group = place // 2, place % 2
         ahead = sublane - lane
         for s in range(2):
-            lhs[s, :, 0:DIM] = keys
             for u in range(4):
                 limit = (own_spans[group * 2 + s] - spans[chunk * 4 + u]) * SPAN
-                lhs[s, u * SPAN : (u + 1) * SPAN, DIM : 2 * DIM] = jnp.where(
+                masks[place, s, u * SPAN : (u + 1) * SPAN, :] = jnp.where(
                     ahead > limit, HIDDEN, 0.0
                 ).astype(BF16)
+        return 0
+
+    lax.fori_loop(0, 16, mask_step, 0)
 
     def load_chunk(chunk):
         keys = kv[pl.ds(chunk * 4, 4), 0].reshape(CHUNK, DIM)
@@ -287,14 +290,15 @@
         def topped(tile):
             cols = pl.ds(tile * WIDE, WIDE)
             s = tile * WIDE // (HEADS * SPAN)
-            score = jnp.dot(lhs[s], qt[group, :, cols], preferred_element_type=F32)
-            sbuf[chunk * 2 + group, :, cols] = score
+            place = chunk * 2 + group
+            masked = jnp.concatenate([keys, masks[place, s]], axis=1)
+            score = jnp.dot(masked, qt[group, :, cols], preferred_element_type=F32)
+            sbuf[place, :, cols] = score
             before = top[group, :, cols]
             now = jnp.maximum(before, jnp.max(fold(score, jnp.max), axis=0, keepdims=True))
             top[group, :, cols] = now
             return now, jnp.exp2((before - now) * exponent)
 
-        masked_keys(chunk, keys, group)
         ahead = topped(0)
         for tile in range(TILES):
             cols = pl.ds(tile * WIDE, WIDE)
@@ -549,7 +553,7 @@
             pltpu.VMEM((2, DIM, COLS), BF16),
             pltpu.VMEM((2, COLS, DIM), BF16),
             pltpu.VMEM((2, COLS, DIM), BF16),
-            pltpu.VMEM((2, CHUNK, 2 * DIM), BF16),
+            pltpu.VMEM((16, 2, CHUNK, SPAN), BF16),
             pltpu.VMEM((16, CHUNK, COLS), F32),
             pltpu.VMEM((CHUNK, COLS), BF16),
             pltpu.VMEM((CHUNK, COLS), BF16),

time: 68.3 us -> 68.1 us (level)
  no operation moved by 1% of the time
where the time goes in v4:
time: 68.1 us; the launch traced here: 68 us
  Pallas kernels  67.4 us (99%)
    pallas_call x1, Pallas kernels, local(): pl.pallas_call(kernel, out_shape=(jax.ShapeDtypeStruct((rows * HEADS, DIM...  65.6 us
    pallas_call x1, Pallas kernels, settled(): pl.pallas_call(settle, out_shape=tuple((jax.ShapeDtypeStruct(r.shape, r.d...  1.74 us

profile of v4, /device:TPU:32, one launch (start us, length us, event | category | flops | bytes accessed | tf_op | source)
XLA Modules:
  0.0 68.0 jit_solution(11201067773584630858)
XLA Ops:
  0.6 65.6 %shard_map.76 = (bf16[1024,128]{1,0:T(8,128)(2,1)}, bf16[256,128]{1,0:T(8,128)(2,1)}, bf16[256,128]{1,0:T(8,128)(2,1)}) custom-call(s32[64]{0:T(128)} %span_ref.1, bf16[1024,128]{1,0:T(8,128)(2,1)} %bitcast.7, bf16[1024,128]{1,0:T(8,128)(2,1)} %bitcast.8, bf16[256,128]{1,0:T(8,128)(2,1)} %bitcast.9, bf16[256,128]{1,0:T(8,128)(2,1)} %bitcast.10), custom_call_target="tpu_custom_call" | custom-call | tf_op jit(solution)/shard_map/pallas_call | solution.py:530
  66.3 1.7 %shard_map.77 = (bf16[1024,128]{1,0:T(8,128)(2,1)}, bf16[256,128]{1,0:T(8,128)(2,1)}, bf16[256,128]{1,0:T(8,128)(2,1)}) custom-call(bf16[1024,128]{1,0:T(8,128)(2,1)} %get-tuple-element.9.refs_0_, bf16[256,128]{1,0:T(8,128)(2,1)} %get-tuple-element.10.refs_1_, bf16[256,128]{1,0:T(8,128)(2,1)} %get-tuple-element.11.refs_2_), custom_call_target="tpu_custom_call" | custom-call | tf_op jit(solution)/shard_map/pallas_call | solution.py:512

commit v5 on v4

--- a/solution.py
+++ b/solution.py
@@ -489,37 +489,26 @@
 
 
 def settle(*refs):
-    count = (len(refs) - 2) // 3
-    sources, targets, held = (refs[i * count : (i + 1) * count] for i in range(3))
-    in_sem, out_sem = refs[-2:]
-    copies = []
-    for i, (source, target, buffer) in enumerate(zip(sources, targets, held)):
-        copies.append((
-            pltpu.make_async_copy(source, buffer, in_sem.at[i]),
-            pltpu.make_async_copy(buffer, target, out_sem.at[i]),
-        ))
-    for inward, _ in copies:
-        inward.start()
-    for inward, outward in copies:
-        inward.wait()
-        outward.start()
-    for _, outward in copies:
-        outward.wait()
+    count = len(refs) // 2
+    sem = refs[-1]
+    copies = [
+        pltpu.make_async_copy(source, target, sem.at[i])
+        for i, (source, target) in enumerate(zip(refs[:count], refs[count : 2 * count]))
+    ]
+    for copy in copies:
+        copy.start()
+    for copy in copies:
+        copy.wait()
 
 
 def settled(*results):
-    anywhere = [pl.BlockSpec(memory_space=pl.ANY)] * len(results)
     return pl.pallas_call(
         settle,
         out_shape=tuple(jax.ShapeDtypeStruct(r.shape, r.dtype) for r in results),
-        in_specs=anywhere,
-        out_specs=tuple(anywhere),
-        scratch_shapes=[
-            *(pltpu.VMEM(r.shape, r.dtype) for r in results),
-            pltpu.SemaphoreType.DMA((len(results),)),
-            pltpu.SemaphoreType.DMA((len(results),)),
-        ],
-    )(*results)
+        in_specs=[pl.BlockSpec(memory_space=pltpu.VMEM)] * len(results),
+        out_specs=tuple([pl.BlockSpec(memory_space=pl.ANY)] * len(results)),
+        scratch_shapes=[pltpu.SemaphoreType.DMA((len(results),))],
+    )(*(pltpu.with_memory_space_constraint(r, pltpu.VMEM) for r in results))
 
 
 def local(queries, key_rows, value_slot_rows, out_grad, span_order):
@@ -530,9 +519,9 @@
     dq, dk, dv = pl.pallas_call(
         kernel,
         out_shape=(
-            jax.ShapeDtypeStruct((rows * HEADS, DIM), BF16),
-            jax.ShapeDtypeStruct((rows, DIM), BF16),
-            jax.ShapeDtypeStruct((rows, DIM), BF16),
+            pltpu.VMEM((rows * HEADS, DIM), BF16),
+            pltpu.VMEM((rows, DIM), BF16),
+            pltpu.VMEM((rows, DIM), BF16),
         ),
         in_specs=[
             pl.BlockSpec(memory_space=pltpu.SMEM),

time: 68.1 us -> 66.4 us (0.975)
  Pallas kernels: 67.4 us -> 65.7 us
    pallas_call x1, Pallas kernels: 1.74 us -> 0.77 us  [settled(): pl.pallas_call(settle, out_shape=tuple((jax.ShapeDtypeStruct(r.shape, r.d...]
    pallas_call x1, Pallas kernels: 65.6 us -> 64.9 us  [local(): pl.pallas_call(kernel, out_shape=(pltpu.VMEM((rows * HEADS, DIM), BF16),...]
where the time goes in v5:
time: 66.4 us; the launch traced here: 66.3 us
  Pallas kernels  65.7 us (99%)
    pallas_call x1, Pallas kernels, local(): pl.pallas_call(kernel, out_shape=(pltpu.VMEM((rows * HEADS, DIM), BF16),...  64.9 us

profile of v5, /device:TPU:32, one launch (start us, length us, event | category | flops | bytes accessed | tf_op | source)
XLA Modules:
  0.0 66.3 jit_solution(4688518918397278937)
XLA Ops:
  0.6 64.9 %shard_map.76 = (bf16[1024,128]{1,0:T(8,128)(2,1)S(1)}, bf16[256,128]{1,0:T(8,128)(2,1)S(1)}, bf16[256,128]{1,0:T(8,128)(2,1)S(1)}) custom-call(s32[64]{0:T(128)} %span_ref.1, bf16[1024,128]{1,0:T(8,128)(2,1)} %bitcast.7, bf16[1024,128]{1,0:T(8,128)(2,1)} %bitcast.8, bf16[256,128]{1,0:T(8,128)(2,1)} %bitcast.9, bf16[256,128]{1,0:T(8,128)(2,1)} %bitcast.10), custom_call_target="tpu_custom_call" | custom-call | tf_op jit(solution)/shard_map/pallas_call | solution.py:519
  65.5 0.8 %shard_map.77 = (bf16[1024,128]{1,0:T(8,128)(2,1)}, bf16[256,128]{1,0:T(8,128)(2,1)}, bf16[256,128]{1,0:T(8,128)(2,1)}) custom-call(bf16[1024,128]{1,0:T(8,128)(2,1)S(1)} %get-tuple-element.9.refs_0_, bf16[256,128]{1,0:T(8,128)(2,1)S(1)} %get-tuple-element.10.refs_1_, bf16[256,128]{1,0:T(8,128)(2,1)S(1)} %get-tuple-element.11.refs_2_), custom_call_target="tpu_custom_call" | custom-call | tf_op jit(solution)/shard_map/pallas_call | solution.py:505
